TPU v7x, 32 devices: a whole 2x2x4 slice. The times are simulated.
32 devices in a mesh: dp: 8 (over z, x), tensor: 4 (over y, core).
Axes of the slice: x: 2, y: 2, z: 4, core: 2. Of those that a mesh axis runs over, the one named last changes fastest.
Arguments:
- tokens: bfloat16 [2048, 8192], P('dp', 'tensor'), may hold values from -6 to 6
- block_routing: int32 [8, 2], replicated, may hold values from -1 to 7, as said below
- frozen_up_weight: bfloat16 [8192, 28672], P('tensor', 'dp'), may hold values from -0.0625 to 0.0625
- adapter_down_weight: bfloat16 [32, 8192], P(None, 'tensor'), may hold values from -0.0625 to 0.0625
- adapter_up_weight: bfloat16 [32, 28672], P(None, 'dp'), may hold values from -6 to 6
- magnitude: float32 [28672], P('dp'), may hold values from 0.5 to 2
- cotangent: bfloat16 [1024, 28672], P('tensor', 'dp'), may hold values from -6 to 6
Outputs:
- projected: bfloat16 [1024, 28672], P('tensor', 'dp')
- grad_a: float32 [32, 8192], P(None, 'tensor')
- grad_b: float32 [32, 28672], P(None, 'dp')
- grad_m: float32 [28672], P('dp')
Inputs may be any that keep to these rules, and one draw needn't show every extreme that they name: `block_routing`: row d lists where the two blocks of dp index d go. Live blocks come first and -1 marks a padding block. A first live block stays on its own index; a second live block goes to index (d + half the dp size) mod the dp size, which then has no live block. Every dp index receives exactly one block. In every draw some index has two live blocks and some has none.
All inputs are finite; a program needn't handle non-finite values.
Results may differ from a plain program's by a relative error of at most 0.018.
Values may be sent and summed in bfloat16 or wider, within the bound.
A program may use at most 128 MiB of HBM per device.

v0:
```python
import functools
import math

import jax
import jax.numpy as jnp
from jax import lax
from jax.experimental import pallas as pl
from jax.experimental.pallas import tpu as pltpu
from jax.sharding import PartitionSpec as P

BLK = 128
ROWS = 16
CHUNKS = BLK // ROWS
HALVES = 2
UNITS = CHUNKS * HALVES
AHEAD = 2
LAG = 2
LANES = 128
MESH = pl.DeviceIdType.MESH
F32 = jnp.float32
BF16 = jnp.bfloat16


def mirrored(value, bits):
    result = 0
    for position in range(bits):
        result = result + (value // (1 << position)) % 2 * (1 << (bits - 1 - position))
    return result


def flipped(value, bit):
    return value + bit - 2 * bit * ((value // bit) % 2)


def dots(left, right, left_dim, right_dim):
    return lax.dot_general(
        left, right, (((left_dim,), (right_dim,)), ((), ())), preferred_element_type=F32
    )


def kernel(
    cfg,
    tok_in, routing, w_hbm, down, up, mag, cot,
    out, ga_out, gb_out, gm_out,
    w, raw, tok, part, near, pair, far, downp, sq, sq_near, sq_far, factor, norm, sg,
    rp, rp_in, rgt, rg, proj_down, gm_acc, gb_part, gb_near, gb_sum, gb_far, gb_all, gm_part, gm_in,
    d_part, d_near, d_pair, d_far,
    w_sem, s0_send, s0_recv, st_send, st_recv, nr_send, nr_recv, fr_send, fr_recv, ms_send, ms_recv,
    dn_send, dn_recv, df_send, df_recv,
):
    dp, tp, width, cols, rank, tile, tps = cfg
    bits = dp.bit_length() - 1
    per = dp // tp
    tiles = cols // tile
    scale = 1.0 / math.sqrt(rank)
    inverse = 1.0 / math.sqrt(dp * BLK)
    d = lax.axis_index("dp")
    t = lax.axis_index("tensor")
    core = t % 2
    side = t // 2
    t_near, t_far = flipped(t, 1), flipped(t, 2)
    hops = [flipped(d, dp >> (k + 1)) for k in range(bits)]

    def copy(src, dst, send, recv, target):
        return pltpu.make_async_remote_copy(
            src_ref=src, dst_ref=dst, send_sem=send, recv_sem=recv,
            device_id=target, device_id_type=MESH,
        )

    def to_dp(k):
        return {"dp": hops[k]}

    near_id, far_id = {"tensor": t_near}, {"tensor": t_far}

    def w_copy(n):
        at = pl.ds(pl.multiple_of(n * tile, tile), tile)
        return pltpu.make_async_copy(w_hbm.at[:, at], w.at[:, at], w_sem.at[n])

    half = width // HALVES

    def lanes(u):
        return pl.ds(pl.multiple_of(u % HALVES * half, half), half)

    def first(u):
        c = u // HALVES
        return copy(
            tok_in.at[:, c, :, lanes(u)], raw.at[c, :, :, lanes(u)],
            s0_send.at[u], s0_recv.at[u], to_dp(0),
        )

    def stage(k, u, owner):
        size = 1 << k
        base = mirrored(owner, bits) // size * size
        rows = pl.ds(pl.multiple_of(base * ROWS, ROWS), size * ROWS)
        here = tok.at[u // HALVES, rows, lanes(u)]
        return copy(here, here, st_send.at[k - 1, u], st_recv.at[k - 1, u], to_dp(k))

    def near_copy(c):
        start = (1 - core) * 2
        return copy(part.at[c, :, pl.ds(start, 2)], near.at[c], nr_send.at[c], nr_recv.at[c], near_id)

    def far_copy(c):
        return copy(pair.at[c], far.at[c], fr_send.at[c], fr_recv.at[c], far_id)

    def down_near(c):
        start = (1 - core) * 2
        return copy(d_part.at[c, :, pl.ds(start, 2)], d_near.at[c], dn_send.at[c], dn_recv.at[c], near_id)

    def down_far(c):
        return copy(d_pair.at[c], d_far.at[c], df_send.at[c], df_recv.at[c], far_id)

    def small(n, src, dst, target):
        return copy(src, dst, ms_send.at[n], ms_recv.at[n], target)

    sq1 = small(0, sq, sq_near, near_id)
    sq2 = small(1, sq_near, sq_far, far_id)
    rp_hops = [small(2 + k, rp.at[k], rp_in.at[k], to_dp(bits - 1 - k)) for k in range(bits)]
    n0 = 2 + bits
    rg1 = small(n0, rgt.at[t], rgt.at[t], near_id)
    rg1_in = small(n0, rgt.at[t_near], rgt.at[t_near], near_id)
    mine2 = pl.ds(side * 2, 2)
    theirs2 = pl.ds((1 - side) * 2, 2)
    rg2 = small(n0 + 1, rgt.at[mine2], rgt.at[mine2], far_id)
    rg2_in = small(n0 + 1, rgt.at[theirs2], rgt.at[theirs2], far_id)

    def each_tile(body):
        @pl.loop(0, tiles)
        def _(n):
            body(pl.ds(pl.multiple_of(n * tile, tile), tile))

    @pl.loop(0, tiles)
    def _(n):
        w_copy(n).start()

    barrier = pltpu.get_barrier_semaphore()
    for k in range(bits):
        pl.semaphore_signal(barrier, inc=1, device_id=to_dp(k), device_id_type=MESH)
    pl.semaphore_signal(barrier, inc=1, device_id=near_id, device_id_type=MESH)
    pl.semaphore_signal(barrier, inc=1, device_id=far_id, device_id_type=MESH)
    pl.semaphore_wait(barrier, bits + 2)

    for c in range(AHEAD):
        first(c).start()
    downp[...] = jnp.zeros_like(downp)
    downp[:rank, :] = down[...]
    gm_acc[...] = jnp.zeros_like(gm_acc)

    own_live = routing[d, 0] == d
    pair_live = routing[hops[0], 0] == hops[0]
    norm_last = (tiles + tps - 1) // tps - 1
    depth = 256

    def norm_tile(n):
        w_copy(n).wait()
        at = pl.ds(pl.multiple_of(n * tile, tile), tile)

        def add(r, total):
            rows = pl.ds(pl.multiple_of(r * depth, depth), depth)
            merged = w[rows, at].astype(F32) + scale * dots(down[:, rows], up[:, at], 0, 0)
            return total + jnp.sum((merged * merged).reshape(depth // 8, 8, tile), axis=0)

        total = lax.fori_loop(0, width // depth, add, jnp.zeros((8, tile), F32))
        sq[:, at] = jnp.sum(total, axis=0, keepdims=True)

    def gradient():
        def body(at):
            square = sq_near[:, at] + sq_far[:, at]
            size = jnp.maximum(jnp.sqrt(square), 0.5)
            ratio = mag[at].reshape(1, tile) / size
            norm[:, at] = size
            factor[:, at] = ratio
            for g in range(per):
                sg[g, :, at] = (cot[g, :, at].astype(F32) * ratio * inverse).astype(BF16)

        each_tile(body)
        for g in range(per):
            rp[0, :, g * BLK:(g + 1) * BLK] = dots(up[...], sg[g], 1, 1)
        rp_hops[0].start()

    def epilogue(c):
        mine = core * 2 + side
        rows = pl.ds(pl.multiple_of(c * ROWS, ROWS), ROWS)
        high = per * ROWS

        def total(at, wide):
            return (
                part[c, :, mine, :, at].astype(F32)
                + near[c, :, side, :, at].astype(F32)
                + far[c, :, :, at].astype(F32)
            ).reshape(high, wide)

        lhs = proj_down[:, rows, :].reshape(high, LANES)[:, :rank]

        def body(at):
            pre = total(at, tile) + scale * jnp.dot(lhs, up[:, at], preferred_element_type=F32)
            out[:, rows, at] = (pre * factor[:, at]).astype(BF16).reshape(per, ROWS, tile)
            both = cot[:, rows, at].astype(F32).reshape(high, tile) * pre
            gm_acc[:, at] += jnp.sum(both.reshape(high // 8, 8, tile), axis=0)

        each_tile(body)

    def when(condition, action):
        pl.when(condition)(action)

    grad_at = norm_last + 2
    gap = max(1, (UNITS + 1 - grad_at) // bits)
    parts = -(-tiles // 2)

    @pl.loop(0, UNITS + LAG * (bits - 1) + 2)
    def _(u):
        when(u + AHEAD < UNITS, lambda: first(u + AHEAD).start())

        @pl.when(u < UNITS)
        def _():
            first(u).wait_recv()
            c = u // HALVES
            at = lanes(u)
            own_at = pl.ds(pl.multiple_of(mirrored(d, bits) * ROWS, ROWS), ROWS)
            pair_at = pl.ds(pl.multiple_of(mirrored(hops[0], bits) * ROWS, ROWS), ROWS)
            tok[c, own_at, at] = jnp.where(own_live, tok_in[0, c, :, at], raw[c, 1, :, at])
            tok[c, pair_at, at] = jnp.where(pair_live, raw[c, 0, :, at], tok_in[1, c, :, at])
            stage(1, u, d).start()

        for k in range(1, bits):
            v = u - LAG * k

            @pl.when((v >= 0) & (v < UNITS))
            def _():
                stage(k, v, hops[k]).wait_recv()
                if k < bits - 1:
                    stage(k + 1, v, d).start()

        @pl.when(u <= norm_last)
        def _():
            for e in range(tps):
                n = u * tps + e
                when(n < tiles, lambda: norm_tile(n))

        when(u == norm_last, lambda: sq1.start())

        @pl.when(u == norm_last + 1)
        def _():
            sq1.wait()
            sq_near[...] = sq_near[...] + sq[...]
            sq2.start()

        @pl.when(u == grad_at)
        def _():
            sq2.wait()
            gradient()

        for k in range(bits):
            @pl.when(u == grad_at + gap * (k + 1))
            def _():
                rp_hops[k].wait()
                merged = rp[k] + rp_in[k]
                if k < bits - 1:
                    rp[k + 1] = merged
                    rp_hops[k + 1].start()
                else:
                    rgt[t] = merged.astype(BF16)
                    rg1.start()

        @pl.when(u == grad_at + gap * bits + 1)
        def _():
            rg1.wait_send()
            rg1_in.wait_recv()
            rg2.start()

        m = u - LAG * (bits - 1) - 1
        j = m // 2
        even = m % 2 == 0

        @pl.when((m >= 2) & even)
        def _():
            c = j - 1
            near_copy(c).wait_recv()
            other = core * 2 + 1 - side

            def body(at):
                pair[c, :, :, at] = (
                    part[c, :, other, :, at].astype(F32)
                    + near[c, :, 1 - side, :, at].astype(F32)
                ).astype(BF16)

            each_tile(body)
            far_copy(c).start()

        @pl.when((m >= 0) & even & (j < CHUNKS))
        def _():
            d_part[j] = dots(tok[j], downp[...], 1, 1).astype(BF16).reshape(per, tp, ROWS, LANES)
            down_near(j).start()

        @pl.when((m >= 0) & (j < CHUNKS))
        def _():
            lhs = tok.at[j]
            begin = (m % 2) * parts

            @pl.loop(0, parts)
            def _(e):
                n = begin + e

                @pl.when(n < tiles)
                def _():
                    at = pl.ds(pl.multiple_of(n * tile, tile), tile)
                    prod = jnp.dot(lhs[...], w[:, at], preferred_element_type=F32)
                    part[j, :, :, :, at] = prod.astype(BF16).reshape(per, tp, ROWS, tile)

        @pl.when((m >= 0) & (m % 2 == 1) & (j < CHUNKS))
        def _():
            near_copy(j).start()
            down_near(j).wait_recv()
            d_pair[j] = (
                d_part[j, :, core * 2 + 1 - side].astype(F32) + d_near[j, :, 1 - side].astype(F32)
            ).astype(BF16)
            down_far(j).start()

        @pl.when((m >= 2) & even)
        def _():
            c = j - 1
            down_far(c).wait_recv()
            rows = pl.ds(pl.multiple_of(c * ROWS, ROWS), ROWS)
            proj_down[:, rows, :] = (
                d_part[c, :, core * 2 + side].astype(F32)
                + d_near[c, :, side].astype(F32)
                + d_far[c].astype(F32)
            ).astype(BF16)

        @pl.when((m >= 5) & (m % 2 == 1))
        def _():
            c = (m - 5) // 2
            far_copy(c).wait_recv()
            epilogue(c)

    n1 = n0 + 2
    share = rank // 2
    gb1 = small(n1, gb_part.at[1 - core], gb_near, near_id)
    gb2 = small(n1 + 1, gb_sum, gb_far, far_id)
    gb3 = small(n1 + 4, gb_all.at[core], gb_all.at[core], near_id)
    gb3_in = small(n1 + 4, gb_all.at[1 - core], gb_all.at[1 - core], near_id)
    gm1 = small(n1 + 2, gm_part.at[0], gm_in.at[0], near_id)
    gm2 = small(n1 + 3, gm_part.at[1], gm_in.at[1], far_id)
    live = proj_down[...].reshape(per * BLK, LANES)[:, :rank]

    def ends(at):
        gb_part[:, :, at] = (
            scale * dots(live, sg[:, :, at].reshape(per * BLK, tile), 0, 0)
        ).astype(BF16).reshape(2, share, tile)

    each_tile(ends)
    gb1.start()

    far_copy(CHUNKS - 2).wait_recv()
    epilogue(CHUNKS - 2)

    gb1.wait()

    def sums(at):
        gb_sum[:, at] = (gb_part[core, :, at].astype(F32) + gb_near[:, at].astype(F32)).astype(BF16)

    each_tile(sums)
    gb2.start()

    rg2.wait_send()
    rg2_in.wait_recv()
    for s in range(tp):
        turned = rgt[s].astype(F32).T.astype(BF16)
        spot = s % 2 * 2 + s // 2
        for g in range(per):
            rg[:, g, spot] = turned[g * BLK:(g + 1) * BLK].reshape(CHUNKS, ROWS, rank)

    wide = min(512, width)

    @pl.loop(0, width // wide)
    def _(n):
        at = pl.ds(pl.multiple_of(n * wide, wide), wide)

        def add(c, total):
            return total + dots(rg[c].reshape(dp * ROWS, rank), tok[c, :, at], 0, 0)

        ga_out[:, at] = scale * lax.fori_loop(0, CHUNKS, add, jnp.zeros((rank, wide), F32))

    far_copy(CHUNKS - 1).wait_recv()
    epilogue(CHUNKS - 1)

    def shares(at):
        gm_part[0, :, at] = (
            jnp.sum(gm_acc[:, at], axis=0, keepdims=True) / norm[:, at] * inverse
        )

    each_tile(shares)
    gm1.start()
    gm1.wait()
    gm_part[1] = gm_part[0] + gm_in[0]
    gm2.start()
    gb2.wait()

    def last(at):
        gb_all[core, :, at] = gb_sum[:, at].astype(F32) + gb_far[:, at].astype(F32)

    each_tile(last)
    gb3.start()
    gm2.wait()
    gm_out[...] = (gm_part[1] + gm_in[1]).reshape(cols)
    gb3.wait_send()
    gb3_in.wait_recv()
    gb_out[...] = gb_all[...].reshape(rank, cols)

    @pl.loop(0, UNITS)
    def _(u):
        first(u).wait_send()
        for k in range(1, bits):
            stage(k, u, d).wait_send()

    @pl.loop(0, CHUNKS)
    def _(c):
        near_copy(c).wait_send()
        far_copy(c).wait_send()
        down_near(c).wait_send()
        down_far(c).wait_send()


def body(dp, tp, tokens, routing, weight, down, up, mag, cot):
    width, cols = weight.shape
    rank = down.shape[0]
    per = dp // tp
    bits = dp.bit_length() - 1
    tile = next(size for size in (512, 256, 128) if cols % size == 0)
    tiles = cols // tile
    tps = -(-tiles // (bits + 1))
    cfg = (dp, tp, width, cols, rank, tile, tps)
    ext = cols
    vmem = pl.BlockSpec(memory_space=pltpu.VMEM)
    dma = pltpu.SemaphoreType.DMA
    mine = per * BLK
    misc = bits + 9
    out, ga, gb, gm = pl.pallas_call(
        functools.partial(kernel, cfg),
        out_shape=(
            jax.ShapeDtypeStruct((per, BLK, cols), BF16),
            jax.ShapeDtypeStruct((rank, width), F32),
            jax.ShapeDtypeStruct((rank, cols), F32),
            jax.ShapeDtypeStruct((cols,), F32),
        ),
        in_specs=[
            vmem,
            pl.BlockSpec(memory_space=pltpu.SMEM),
            pl.BlockSpec(memory_space=pl.ANY),
            vmem, vmem, vmem, vmem,
        ],
        out_specs=(vmem, vmem, vmem, vmem),
        scratch_shapes=[
            pltpu.VMEM((width, cols), BF16),
            pltpu.VMEM((CHUNKS, 2, ROWS, width), BF16),
            pltpu.VMEM((CHUNKS, dp * ROWS, width), BF16),
            pltpu.VMEM((CHUNKS, per, tp, ROWS, ext), BF16),
            pltpu.VMEM((CHUNKS, per, 2, ROWS, ext), BF16),
            pltpu.VMEM((CHUNKS, per, ROWS, ext), BF16),
            pltpu.VMEM((CHUNKS, per, ROWS, ext), BF16),
            pltpu.VMEM((LANES, width), BF16),
            pltpu.VMEM((1, cols), F32),
            pltpu.VMEM((1, cols), F32),
            pltpu.VMEM((1, cols), F32),
            pltpu.VMEM((1, cols), F32),
            pltpu.VMEM((1, cols), F32),
            pltpu.VMEM((per, BLK, cols), BF16),
            pltpu.VMEM((bits, rank, mine), F32),
            pltpu.VMEM((bits, rank, mine), F32),
            pltpu.VMEM((tp, rank, mine), BF16),
            pltpu.VMEM((CHUNKS, per, tp, ROWS, rank), BF16),
            pltpu.VMEM((per, BLK, LANES), BF16),
            pltpu.VMEM((8, cols), F32),
            pltpu.VMEM((2, rank // 2, cols), BF16),
            pltpu.VMEM((rank // 2, cols), BF16),
            pltpu.VMEM((rank // 2, cols), BF16),
            pltpu.VMEM((rank // 2, cols), BF16),
            pltpu.VMEM((2, rank // 2, cols), F32),
            pltpu.VMEM((2, 1, cols), F32),
            pltpu.VMEM((2, 1, cols), F32),
            pltpu.VMEM((CHUNKS, per, tp, ROWS, LANES), BF16),
            pltpu.VMEM((CHUNKS, per, 2, ROWS, LANES), BF16),
            pltpu.VMEM((CHUNKS, per, ROWS, LANES), BF16),
            pltpu.VMEM((CHUNKS, per, ROWS, LANES), BF16),
            dma((tiles,)),
            dma((UNITS,)), dma((UNITS,)),
            dma((bits - 1, UNITS)), dma((bits - 1, UNITS)),
            dma((CHUNKS,)), dma((CHUNKS,)),
            dma((CHUNKS,)), dma((CHUNKS,)),
            dma((misc,)), dma((misc,)),
            dma((CHUNKS,)), dma((CHUNKS,)),
            dma((CHUNKS,)), dma((CHUNKS,)),
        ],
        compiler_params=pltpu.CompilerParams(
            collective_id=0, has_side_effects=True, vmem_limit_bytes=67043328
        ),
    )(
        tokens.reshape(2, CHUNKS, ROWS, width),
        routing,
        weight,
        down,
        up,
        mag,
        cot.reshape(per, BLK, cols),
    )
    return out.reshape(mine, cols), ga, gb, gm


def solution(mesh):
    return jax.shard_map(
        functools.partial(body, mesh.shape["dp"], mesh.shape["tensor"]),
        mesh=mesh,
        in_specs=(
            P("dp", "tensor"),
            P(),
            P("tensor", "dp"),
            P(None, "tensor"),
            P(None, "dp"),
            P("dp"),
            P("tensor", "dp"),
        ),
        out_specs=(P("tensor", "dp"), P(None, "tensor"), P(None, "dp"), P("dp")),
        check_vma=False,
    )
```

profile of v0, /device:TPU:0, one launch (start us, length us, event | category | flops | bytes accessed | tf_op | source)
XLA Modules:
  0.0 104.4 jit_solution(17511962856952761503)
XLA Ops:
  0.6 1.3 %copy.11.routing = s32[8,2]{1,0:T(8,128)} copy(s32[8,2]{0,1:T(2,128)} %param.8) | data formatting | bytes 128 | tf_op args[1]
  2.0 97.4 %shard_map.102 = (bf16[2,128,3584]{2,1,0:T(8,128)(2,1)}, f32[32,2048]{1,0:T(8,128)}, f32[32,3584]{1,0:T(8,128)}, f32[3584]{0:T(1024)}) custom-call(bf16[2,8,16,2048]{3,2,1,0:T(8,128)(2,1)} %bitcast.5, s32[8,2]{1,0:T(8,128)} %copy.11.routing, bf16[2048,3584]{1,0:T(8,128)(2,1)} %w_hbm.1, bf16[32,2048]{1,0:T(8,128)(2,1)} %down.1, bf16[32,3584]{1,0:T(8,128)(2,1)} %up.1, ...), custom_call_target="tpu_custom_call" | custom-call | tf_op jit(solution)/shard_map/pallas_call | solution.py:437
  99.3 0.0 copy-start.1
  99.4 0.0 copy-start
  99.4 0.0 copy-start.2
  99.4 2.9 %copy.16 = bf16[256,3584]{1,0:T(8,128)(2,1)} copy(bf16[256,3584]{1,0:T(8,128)(2,1)} %bitcast.4) | data formatting | bytes 3670016
  102.3 0.0 copy-done.1
  102.3 0.7 copy.17
  103.0 0.0 copy-done
  103.0 0.8 copy.18
  103.8 0.0 copy-done.2
  103.8 0.6 copy.19
Async XLA Ops:
  99.3 2.9 %copy-start.1 = (f32[32,2048]{1,0:T(8,128)S(1)}, f32[32,2048]{1,0:T(8,128)}, u32[]{:S(2)}) copy-start(f32[32,2048]{1,0:T(8,128)} %get-tuple-element.17) | copy-start | bytes 786436
  99.4 3.6 %copy-start = (f32[32,3584]{1,0:T(8,128)S(1)}, f32[32,3584]{1,0:T(8,128)}, u32[]{:S(2)}) copy-start(f32[32,3584]{1,0:T(8,128)} %get-tuple-element.18) | copy-start | bytes 1376260
  99.4 4.4 %copy-start.2 = (f32[3584]{0:T(1024)S(1)}, f32[3584]{0:T(1024)}, u32[]{:S(2)}) copy-start(f32[3584]{0:T(1024)} %get-tuple-element.19) | copy-start | bytes 43012
where the time goes:
time: 105 us; the launch traced here: 104 us
  Pallas kernels  97.4 us (93%)
  local copies, waits for them, and re-layouts  6.35 us (6%)
    pallas_call x1, Pallas kernels, body(): pl.pallas_call(functools.partial(kernel, cfg), out_shape=(jax.ShapeDtypeS...  97.4 us
    unnamed x11, local copies, waits for them, and re-layouts  6.35 us

commit v1 on v0

v1 whole, which is shorter than its diff:
```python
import functools
import math

import jax
import jax.numpy as jnp
from jax import lax
from jax.experimental import pallas as pl
from jax.experimental.pallas import tpu as pltpu
from jax.sharding import PartitionSpec as P

BLK = 128
ROWS = 16
CHUNKS = BLK // ROWS
HALVES = 2
UNITS = CHUNKS * HALVES
AHEAD = 2
LAG = 2
EARLY = 3
LANES = 128
MESH = pl.DeviceIdType.MESH
F32 = jnp.float32
BF16 = jnp.bfloat16


def mirrored(value, bits):
    result = 0
    for position in range(bits):
        result = result + (value // (1 << position)) % 2 * (1 << (bits - 1 - position))
    return result


def flipped(value, bit):
    return value + bit - 2 * bit * ((value // bit) % 2)


def dots(left, right, left_dim, right_dim):
    return lax.dot_general(
        left, right, (((left_dim,), (right_dim,)), ((), ())), preferred_element_type=F32
    )


def kernel(
    cfg,
    tok_hbm, routing, w_hbm, down_hbm, up_hbm, mag_hbm, cot_hbm,
    out, ga_out, gb_out, gm_out,
    tok_in, down, up, mag, cot, w,
    raw, tok, part, near, pair, far, sq, sq_near, sq_far, factor, norm, sg,
    rp, rp_in, rgt, rg, rg_turned, proj_down, proj_turned, gm_acc,
    gb_part, gb_near, gb_sum, gb_far, gb_all, gm_in, d_loc, d_in, d_all,
    in_sem, w_sem, s0_send, s0_recv, st_send, st_recv, nr_send, nr_recv, fr_send, fr_recv,
    ms_send, ms_recv, ds_send, ds_recv, db_send, db_recv, gm_send, gm_recv,
):
    dp, tp, width, cols, rank, tile = cfg
    bits = dp.bit_length() - 1
    per = dp // tp
    tiles = cols // tile
    cut = (tiles + 1) // 2
    pieces = ((0, cut), (cut, tiles))
    order = [mirrored(g, per.bit_length() - 1) for g in range(per)]
    scale = 1.0 / math.sqrt(rank)
    inverse = 1.0 / math.sqrt(dp * BLK)
    high = per * ROWS
    d = lax.axis_index("dp")
    t = lax.axis_index("tensor")
    core = t % 2
    side = t // 2
    t_near, t_far = flipped(t, 1), flipped(t, 2)
    hops = [flipped(d, dp >> (k + 1)) for k in range(bits)]
    homes = (d // per, hops[0] // per)

    def copy(src, dst, send, recv, target):
        return pltpu.make_async_remote_copy(
            src_ref=src, dst_ref=dst, send_sem=send, recv_sem=recv,
            device_id=target, device_id_type=MESH,
        )

    def when(condition, action):
        pl.when(condition)(action)

    def to_dp(k):
        return {"dp": hops[k]}

    near_id, far_id = {"tensor": t_near}, {"tensor": t_far}

    def span(p):
        return pl.ds(pieces[p][0] * tile, (pieces[p][1] - pieces[p][0]) * tile)

    def tile_at(n):
        if isinstance(n, int):
            return pl.ds(n * tile, tile)
        return pl.ds(pl.multiple_of(n * tile, tile), tile)

    def w_copy(n):
        return pltpu.make_async_copy(w_hbm.at[:, tile_at(n)], w.at[:, tile_at(n)], w_sem.at[n])

    tok_copy = pltpu.make_async_copy(tok_hbm, tok_in, in_sem.at[0])
    loads = [
        pltpu.make_async_copy(down_hbm, down, in_sem.at[1]),
        pltpu.make_async_copy(up_hbm, up, in_sem.at[2]),
        pltpu.make_async_copy(mag_hbm, mag, in_sem.at[3]),
    ]
    cot_loads = [
        pltpu.make_async_copy(cot_hbm.at[g], cot.at[order[g]], in_sem.at[4 + g])
        for g in range(per)
    ]

    half = width // HALVES

    def lanes(h):
        return pl.ds(h * half, half)

    def first(u, h):
        c = u // HALVES
        return copy(
            tok_in.at[:, c, :, lanes(h)], raw.at[c, :, :, lanes(h)],
            s0_send.at[u], s0_recv.at[u], to_dp(0),
        )

    def stage(k, u, h, owner):
        size = 1 << k
        base = mirrored(owner, bits) // size * size
        rows = pl.ds(pl.multiple_of(base * ROWS, ROWS), size * ROWS)
        here = tok.at[u // HALVES, rows, lanes(h)]
        return copy(here, here, st_send.at[k - 1, u], st_recv.at[k - 1, u], to_dp(k))

    def near_copy(c, p):
        start = (1 - core) * 2
        return copy(
            part.at[c, :, pl.ds(start, 2), :, span(p)], near.at[c, :, :, :, span(p)],
            nr_send.at[c, p], nr_recv.at[c, p], near_id,
        )

    def far_copy(c, p):
        return copy(
            pair.at[c, :, :, span(p)], far.at[c, :, :, span(p)],
            fr_send.at[c, p], fr_recv.at[c, p], far_id,
        )

    def home_copy(s):
        return copy(
            d_loc.at[s], d_in.at[s, t], ds_send.at[s], ds_recv.at[s, t], {"tensor": homes[s]}
        )

    def home_in(s, other):
        return copy(
            d_in.at[s, other], d_in.at[s, other], ds_send.at[s], ds_recv.at[s, other], near_id
        )

    def spread(s, k):
        return copy(
            d_all.at[s, d], d_all.at[s, d], db_send.at[k], db_recv.at[s, d], {"dp": (d + k) % dp}
        )

    def spread_in(s, source):
        return copy(
            d_all.at[s, source], d_all.at[s, source], db_send.at[0], db_recv.at[s, source],
            {"dp": hops[0]},
        )

    def gm_copy(k):
        return copy(
            gm_in.at[t], gm_in.at[t], gm_send.at[k], gm_recv.at[t], {"tensor": (t + k) % tp}
        )

    def gm_from(k):
        source = (t + k) % tp
        return copy(
            gm_in.at[source], gm_in.at[source], gm_send.at[k], gm_recv.at[source], near_id
        )

    def small(n, src, dst, target):
        return copy(src, dst, ms_send.at[n], ms_recv.at[n], target)

    sq1 = small(0, sq, sq_near, near_id)
    sq2 = small(1, sq_near, sq_far, far_id)
    rp_hops = [small(2 + k, rp.at[k], rp_in.at[k], to_dp(bits - 1 - k)) for k in range(bits)]
    n0 = 2 + bits
    rg1 = small(n0, rgt.at[t], rgt.at[t], near_id)
    rg1_in = small(n0, rgt.at[t_near], rgt.at[t_near], near_id)
    mine2 = pl.ds(side * 2, 2)
    theirs2 = pl.ds((1 - side) * 2, 2)
    rg2 = small(n0 + 1, rgt.at[mine2], rgt.at[mine2], far_id)
    rg2_in = small(n0 + 1, rgt.at[theirs2], rgt.at[theirs2], far_id)
    share = rank // 2
    gb1 = small(n0 + 2, gb_part.at[1 - core], gb_near, near_id)
    gb2 = small(n0 + 3, gb_sum, gb_far, far_id)
    gb3 = small(n0 + 4, gb_all.at[core], gb_all.at[core], near_id)
    gb3_in = small(n0 + 4, gb_all.at[1 - core], gb_all.at[1 - core], near_id)

    def each_tile(body):
        @pl.loop(0, tiles)
        def _(n):
            body(tile_at(n))

    barrier = pltpu.get_barrier_semaphore()

    def greet_dp(k):
        pl.semaphore_signal(barrier, inc=1, device_id={"dp": (d + k) % dp}, device_id_type=MESH)

    @pl.loop(1, dp)
    def _(k):
        greet_dp(k)

    for k in range(1, tp):
        pl.semaphore_signal(barrier, inc=1, device_id={"tensor": (t + k) % tp}, device_id_type=MESH)

    tok_copy.start()
    for load in loads:
        load.start()
    for n in range(tiles):
        w_copy(n).start()
    for load in cot_loads:
        load.start()

    gm_acc[...] = jnp.zeros_like(gm_acc)
    tok_copy.wait()
    pl.semaphore_wait(barrier, dp - 1 + tp - 1)
    for u in range(AHEAD):
        first(u, u % HALVES).start()
    for load in loads:
        load.wait()

    for s in range(2):
        block = tok_in[s].reshape(BLK, width)
        d_loc[s] = dots(down[...], block, 1, 1).astype(BF16)
    for s in range(2):
        when(t != homes[s], lambda: home_copy(s).start())

    gram = dots(down[...], down[...], 1, 1)
    gram_high = gram.astype(BF16)
    gram_low = (gram - gram_high.astype(F32)).astype(BF16)

    own_live = routing[0, d] == d
    pair_live = routing[0, hops[0]] == hops[0]
    depth = 256

    def norm_tile(n):
        w_copy(n).wait()
        at = tile_at(n)
        cross = jnp.dot(down[...], w[:, at], preferred_element_type=F32)
        total = jnp.zeros((16, tile), F32)
        for r in range(0, width, depth):
            block = w[r:r + depth, at].astype(F32)
            total = total + jnp.sum((block * block).reshape(depth // 16, 16, tile), axis=0)
        ups = up[:, at]
        quad = (
            jnp.dot(gram_high, ups, preferred_element_type=F32)
            + jnp.dot(gram_low, ups, preferred_element_type=F32)
        )
        mixed = (2.0 * scale * cross + scale * scale * quad) * ups.astype(F32)
        sq[:, at] = (
            jnp.sum(total, axis=0, keepdims=True) + jnp.sum(mixed, axis=0, keepdims=True)
        )

    def gradient():
        def body(at):
            square = sq_near[:, at] + sq_far[:, at]
            size = jnp.sqrt(jnp.maximum(square, 0.25))
            ratio = mag[at].reshape(1, tile) / size
            norm[:, at] = size
            factor[:, at] = ratio
            for g in range(per):
                sg[g, :, at] = (cot[g, :, at].astype(F32) * ratio * inverse).astype(BF16)

        each_tile(body)
        for g in range(per):
            rp[0, :, g * BLK:(g + 1) * BLK] = dots(up[...], sg[g], 1, 1)

    def gather_down():
        for s in range(2):
            @pl.when(t == homes[s])
            def _():
                d_in[s, t] = d_loc[s]
                for k in range(1, tp):
                    home_in(s, (t + k) % tp).wait_recv()
                total = d_in[s, 0].astype(F32)
                for other in range(1, tp):
                    total = total + d_in[s, other].astype(F32)
                d_all[s, d] = total.astype(BF16)

                @pl.loop(1, dp)
                def _(k):
                    spread(s, k).start()

    def take_down():
        for g in range(per):
            p = t * per + g
            across = flipped(p, dp // 2)
            when(p != d, lambda: spread_in(0, p).wait_recv())
            when(across != d, lambda: spread_in(1, across).wait_recv())
            live = routing[0, p] == p
            turned = jnp.where(live, d_all[0, p], d_all[1, across])
            proj_turned[:, order[g] * BLK:(order[g] + 1) * BLK] = turned
            proj_down[order[g]] = turned.astype(F32).T.astype(BF16)

    def multiply(c, p):
        for n in range(*pieces[p]):
            at = tile_at(n)
            prod = jnp.dot(tok[c], w[:, at], preferred_element_type=F32)
            part[c, :, :, :, at] = prod.astype(BF16).reshape(per, tp, ROWS, tile)
        near_copy(c, p).start()

    def combine(c, p):
        near_copy(c, p).wait_recv()
        other = core * 2 + 1 - side
        for n in range(*pieces[p]):
            at = tile_at(n)
            pair[c, :, :, at] = (
                part[c, :, other, :, at].astype(F32) + near[c, :, 1 - side, :, at].astype(F32)
            ).astype(BF16)
        far_copy(c, p).start()

    def epilogue(c, p):
        far_copy(c, p).wait_recv()
        mine = core * 2 + side
        rows = pl.ds(pl.multiple_of(c * ROWS, ROWS), ROWS)
        lhs = proj_down[:, rows, :].reshape(high, rank)
        for n in range(*pieces[p]):
            at = tile_at(n)
            total = (
                part[c, :, mine, :, at].astype(F32)
                + near[c, :, side, :, at].astype(F32)
                + far[c, :, :, at].astype(F32)
            ).reshape(high, tile)
            pre = total + scale * jnp.dot(lhs, up[:, at], preferred_element_type=F32)
            out[:, rows, at] = (pre * factor[:, at]).astype(BF16).reshape(per, ROWS, tile)
            both = cot[:, rows, at].astype(F32).reshape(high, tile) * pre
            gm_acc[:, at] += jnp.sum(both.reshape(high // 8, 8, tile), axis=0)

    def gb_start():
        for n in range(tiles):
            at = tile_at(n)
            gb_part[:, :, at] = (
                scale * jnp.dot(
                    proj_turned[...], sg[:, :, at].reshape(per * BLK, tile),
                    preferred_element_type=F32,
                )
            ).astype(BF16).reshape(2, share, tile)
        gb1.start()

    def turn_rows():
        for s in range(tp):
            turned = rgt[s].astype(F32).T.astype(BF16)
            spot = s % 2 * 2 + s // 2
            for g in range(per):
                rg[:, g, spot] = turned[g * BLK:(g + 1) * BLK].reshape(CHUNKS, ROWS, rank)
        rg_turned[...] = rg[...].reshape(dp * BLK, rank).astype(F32).T.astype(BF16)

    for n in range(min(EARLY, tiles)):
        norm_tile(n)

    later = max(0, tiles - EARLY)
    norm_last = -(-later // 2)
    grad_at = norm_last + 2
    gap = max(1, (UNITS - grad_at) // (bits + 1))
    ready = LAG * (bits - 1) + 1
    steps = UNITS + ready + 1
    steps = steps + steps % 2
    gb_at = ready + 3

    @pl.loop(0, steps // 2)
    def _(pass_):
        for h in range(2):
            u = pass_ * 2 + h

            @pl.when(u < UNITS)
            def _():
                first(u, h).wait_recv()
                c = u // HALVES
                at = lanes(h)
                own_at = pl.ds(pl.multiple_of(mirrored(d, bits) * ROWS, ROWS), ROWS)
                pair_at = pl.ds(pl.multiple_of(mirrored(hops[0], bits) * ROWS, ROWS), ROWS)
                tok[c, own_at, at] = jnp.where(own_live, tok_in[0, c, :, at], raw[c, 1, :, at])
                tok[c, pair_at, at] = jnp.where(pair_live, raw[c, 0, :, at], tok_in[1, c, :, at])
                stage(1, u, h, d).start()

            when(u + AHEAD < UNITS, lambda: first(u + AHEAD, (h + AHEAD) % 2).start())

            for k in range(1, bits):
                v = u - LAG * k
                hv = (h - LAG * k) % 2

                @pl.when((v >= 0) & (v < UNITS))
                def _():
                    stage(k, v, hv, hops[k]).wait_recv()
                    if k < bits - 1:
                        stage(k + 1, v, hv, d).start()

            @pl.when((u >= 1) & (u <= norm_last))
            def _():
                for e in range(2):
                    n = EARLY + (u - 1) * 2 + e
                    when(n < tiles, lambda: norm_tile(n))

            when(u == 1, gather_down)
            when(u == norm_last, lambda: sq1.start())

            @pl.when(u == norm_last + 1)
            def _():
                sq1.wait()
                sq_near[...] = sq_near[...] + sq[...]
                sq2.start()

            @pl.when(u == grad_at)
            def _():
                sq2.wait()
                for load in cot_loads:
                    load.wait()
                gradient()
                rp_hops[0].start()

            when(u == ready, take_down)

            for k in range(bits):
                @pl.when(u == grad_at + gap * (k + 1))
                def _():
                    rp_hops[k].wait()
                    merged = rp[k] + rp_in[k]
                    if k < bits - 1:
                        rp[k + 1] = merged
                        rp_hops[k + 1].start()
                    else:
                        rgt[t] = merged.astype(BF16)
                        rg1.start()

            @pl.when(u == grad_at + gap * bits + 1)
            def _():
                rg1.wait_send()
                rg1_in.wait_recv()
                rg2.start()

            @pl.when(u == grad_at + gap * bits + 3)
            def _():
                rg2.wait_send()
                rg2_in.wait_recv()
                turn_rows()

            m = u - ready
            hm = (h - ready) % 2
            when((m >= 0) & (m < UNITS), lambda: multiply(m // 2, hm))
            when((m >= 1) & (m <= UNITS), lambda: combine((m - 1) // 2, 1 - hm))
            when((m >= 3) & (m <= UNITS), lambda: epilogue((m - 3) // 2, 1 - hm))

            when(u == gb_at, gb_start)

            @pl.when(u == gb_at + 2)
            def _():
                gb1.wait()
                gb_sum[...] = (gb_part[core].astype(F32) + gb_near[...].astype(F32)).astype(BF16)
                gb2.start()

            @pl.when(u == gb_at + 6)
            def _():
                gb2.wait()
                gb_all[core] = gb_sum[...].astype(F32) + gb_far[...].astype(F32)
                gb3.start()

            @pl.when(u == gb_at + 8)
            def _():
                gb3.wait_send()
                gb3_in.wait_recv()
                gb_out[...] = gb_all[...].reshape(rank, cols)

    wide = min(512, width)

    @pl.loop(0, width // wide)
    def _(n):
        at = pl.ds(pl.multiple_of(n * wide, wide), wide)
        ga_out[:, at] = scale * jnp.dot(
            rg_turned[...], tok[:, :, at].reshape(dp * BLK, wide), preferred_element_type=F32
        )

    @pl.loop(0, CHUNKS)
    def _(c):
        for h in range(HALVES):
            u = c * HALVES + h
            first(u, h).wait_send()
            for k in range(1, bits):
                stage(k, u, h, d).wait_send()
        for p in range(2):
            near_copy(c, p).wait_send()

    for s in range(2):
        when(t != homes[s], lambda: home_copy(s).wait_send())

        @pl.when(t == homes[s])
        def _():
            @pl.loop(1, dp)
            def _(k):
                spread(s, k).wait_send()

    for q in range(UNITS - 2, UNITS):
        epilogue(q // 2, q % 2)

    gm_in[t] = jnp.sum(gm_acc[...], axis=0, keepdims=True) / norm[...] * inverse
    for k in range(1, tp):
        gm_copy(k).start()

    @pl.loop(0, CHUNKS)
    def _(c):
        for p in range(2):
            far_copy(c, p).wait_send()

    for k in range(1, tp):
        gm_from(k).wait_recv()
    total = gm_in[0]
    for s in range(1, tp):
        total = total + gm_in[s]
    gm_out[...] = total.reshape(cols)
    for k in range(1, tp):
        gm_copy(k).wait_send()


def finish(order, out, ga, gb, gm, out_hbm, ga_hbm, gb_hbm, gm_hbm, sem):
    moves = [
        pltpu.make_async_copy(out.at[order[g]], out_hbm.at[g], sem.at[g])
        for g in range(len(order))
    ]
    for src, dst in ((ga, ga_hbm), (gb, gb_hbm), (gm, gm_hbm)):
        moves.append(pltpu.make_async_copy(src, dst, sem.at[len(moves)]))
    for move in moves:
        move.start()
    for move in moves:
        move.wait()


def body(dp, tp, tokens, routing, weight, down, up, mag, cot):
    width, cols = weight.shape
    rank = down.shape[0]
    per = dp // tp
    bits = dp.bit_length() - 1
    tile = next(size for size in (512, 256, 128) if cols % size == 0)
    tiles = cols // tile
    cfg = (dp, tp, width, cols, rank, tile)
    vmem = pl.BlockSpec(memory_space=pltpu.VMEM)
    hbm = pl.BlockSpec(memory_space=pltpu.HBM)
    dma = pltpu.SemaphoreType.DMA
    mine = per * BLK
    shapes = (
        ((per, BLK, cols), BF16),
        ((rank, width), F32),
        ((rank, cols), F32),
        ((cols,), F32),
    )
    held = pl.pallas_call(
        functools.partial(kernel, cfg),
        out_shape=tuple(OUT(shape, kind) for shape, kind in shapes),
        in_specs=[hbm, pl.BlockSpec(memory_space=pltpu.SMEM), hbm, hbm, hbm, hbm, hbm],
        out_specs=(vmem, vmem, vmem, vmem),
        scratch_shapes=[
            pltpu.VMEM((2, CHUNKS, ROWS, width), BF16),
            pltpu.VMEM((rank, width), BF16),
            pltpu.VMEM((rank, cols), BF16),
            pltpu.VMEM((cols,), F32),
            pltpu.VMEM((per, BLK, cols), BF16),
            pltpu.VMEM((width, cols), BF16),
            pltpu.VMEM((CHUNKS, 2, ROWS, width), BF16),
            pltpu.VMEM((CHUNKS, dp * ROWS, width), BF16),
            pltpu.VMEM((CHUNKS, per, tp, ROWS, cols), BF16),
            pltpu.VMEM((CHUNKS, per, 2, ROWS, cols), BF16),
            pltpu.VMEM((CHUNKS, per, ROWS, cols), BF16),
            pltpu.VMEM((CHUNKS, per, ROWS, cols), BF16),
            pltpu.VMEM((1, cols), F32),
            pltpu.VMEM((1, cols), F32),
            pltpu.VMEM((1, cols), F32),
            pltpu.VMEM((1, cols), F32),
            pltpu.VMEM((1, cols), F32),
            pltpu.VMEM((per, BLK, cols), BF16),
            pltpu.VMEM((bits, rank, mine), F32),
            pltpu.VMEM((bits, rank, mine), F32),
            pltpu.VMEM((tp, rank, mine), BF16),
            pltpu.VMEM((CHUNKS, per, tp, ROWS, rank), BF16),
            pltpu.VMEM((rank, dp * BLK), BF16),
            pltpu.VMEM((per, BLK, rank), BF16),
            pltpu.VMEM((rank, mine), BF16),
            pltpu.VMEM((8, cols), F32),
            pltpu.VMEM((2, rank // 2, cols), BF16),
            pltpu.VMEM((rank // 2, cols), BF16),
            pltpu.VMEM((rank // 2, cols), BF16),
            pltpu.VMEM((rank // 2, cols), BF16),
            pltpu.VMEM((2, rank // 2, cols), F32),
            pltpu.VMEM((tp, 1, cols), F32),
            pltpu.VMEM((2, rank, BLK), BF16),
            pltpu.VMEM((2, tp, rank, BLK), BF16),
            pltpu.VMEM((2, dp, rank, BLK), BF16),
            dma((4 + per,)),
            dma((tiles,)),
            dma((UNITS,)), dma((UNITS,)),
            dma((bits - 1, UNITS)), dma((bits - 1, UNITS)),
            dma((CHUNKS, 2)), dma((CHUNKS, 2)),
            dma((CHUNKS, 2)), dma((CHUNKS, 2)),
            dma((bits + 7,)), dma((bits + 7,)),
            dma((2,)), dma((2, tp)),
            dma((dp,)), dma((2, dp)),
            dma((tp,)), dma((tp,)),
        ],
        compiler_params=pltpu.CompilerParams(
            collective_id=0, has_side_effects=True, vmem_limit_bytes=LIMIT
        ),
    )(
        tokens.reshape(2, CHUNKS, ROWS, width),
        routing.T,
        weight,
        down,
        up,
        mag,
        cot.reshape(per, BLK, cols),
    )
    order = [mirrored(g, per.bit_length() - 1) for g in range(per)]
    out, ga, gb, gm = pl.pallas_call(
        functools.partial(finish, order),
        out_shape=tuple(jax.ShapeDtypeStruct(shape, kind) for shape, kind in shapes),
        in_specs=[vmem, vmem, vmem, vmem],
        out_specs=(hbm, hbm, hbm, hbm),
        scratch_shapes=[dma((per + 3,))],
    )(*(pltpu.with_memory_space_constraint(x, pltpu.VMEM) for x in held))
    return out.reshape(mine, cols), ga, gb, gm


OUT = pltpu.VMEM
LIMIT = 56 * 1024 * 1024


def solution(mesh):
    return jax.shard_map(
        functools.partial(body, mesh.shape["dp"], mesh.shape["tensor"]),
        mesh=mesh,
        in_specs=(
            P("dp", "tensor"),
            P(),
            P("tensor", "dp"),
            P(None, "tensor"),
            P(None, "dp"),
            P("dp"),
            P("tensor", "dp"),
        ),
        out_specs=(P("tensor", "dp"), P(None, "tensor"), P(None, "dp"), P("dp")),
        check_vma=False,
    )
```

time: 105 us -> 85.6 us (0.82)
  Pallas kernels: 97.4 us -> 84.8 us
  local copies, waits for them, and re-layouts: 6.35 us -> 0 us
    pallas_call x1 -> x2, Pallas kernels: 97.4 us -> 84.8 us  [the longest x1 83.3 us: body(): pl.pallas_call(functools.partial(kernel, cfg), out_shape=tuple((OUT(shape...]
    unnamed x11 -> x0, local copies, waits for them, and re-layouts: 6.35 us -> none
where the time goes in v1:
time: 85.6 us; the launch traced here: 85.5 us
  Pallas kernels  84.8 us (99%)
    pallas_call x1, Pallas kernels, body(): pl.pallas_call(functools.partial(kernel, cfg), out_shape=tuple((OUT(shape...  83.3 us

profile of v1, /device:TPU:0, one launch (start us, length us, event | category | flops | bytes accessed | tf_op | source)
XLA Modules:
  0.0 85.5 jit_solution(14868443031665371284)
XLA Ops:
  0.6 83.3 %shard_map.102 = (bf16[2,128,3584]{2,1,0:T(8,128)(2,1)S(1)}, f32[32,2048]{1,0:T(8,128)S(1)}, f32[32,3584]{1,0:T(8,128)S(1)}, f32[3584]{0:T(1024)S(1)}) custom-call(bf16[2,8,16,2048]{3,2,1,0:T(8,128)(2,1)} %bitcast.5, s32[2,8]{1,0:T(2,128)} %bitcast.6, bf16[2048,3584]{1,0:T(8,128)(2,1)} %w_hbm.1, bf16[32,2048]{1,0:T(8,128)(2,1)} %down_hbm.1, ...), custom_call_target="tpu_custom_call" | custom-call | tf_op jit(solution)/shard_map/pallas_call | solution.py:545
  83.9 1.5 %shard_map.103 = (bf16[2,128,3584]{2,1,0:T(8,128)(2,1)}, f32[32,2048]{1,0:T(8,128)}, f32[32,3584]{1,0:T(8,128)}, f32[3584]{0:T(1024)}) custom-call(bf16[2,128,3584]{2,1,0:T(8,128)(2,1)S(1)} %get-tuple-element.12.out, f32[32,2048]{1,0:T(8,128)S(1)} %get-tuple-element.13.ga, f32[32,3584]{1,0:T(8,128)S(1)} %get-tuple-element.14.gb, f32[3584]{0:T(1024)S(1)} %get-tuple-element.15.gm), custom_call_target="tpu_custom_call" | custom-call | tf_op jit(solution)/shard_map/pallas_call | solution.py:610

commit v2 on v1

--- a/solution.py
+++ b/solution.py
@@ -11,12 +11,14 @@
 BLK = 128
 ROWS = 16
 CHUNKS = BLK // ROWS
-HALVES = 2
+HALVES = 4
 UNITS = CHUNKS * HALVES
-AHEAD = 2
-LAG = 2
+AHEAD = 4
+LAG = 3
 EARLY = 3
-LANES = 128
+PAIR_LAG = 1
+END_LAG = 4
+RING = HALVES * -(-(2 * max(AHEAD, LAG, PAIR_LAG, END_LAG) + 2) // HALVES)
 MESH = pl.DeviceIdType.MESH
 F32 = jnp.float32
 BF16 = jnp.bfloat16
@@ -54,8 +56,8 @@
     bits = dp.bit_length() - 1
     per = dp // tp
     tiles = cols // tile
-    cut = (tiles + 1) // 2
-    pieces = ((0, cut), (cut, tiles))
+    cut = -(-tiles // HALVES)
+    pieces = [(min(p * cut, tiles), min((p + 1) * cut, tiles)) for p in range(HALVES)]
     order = [mirrored(g, per.bit_length() - 1) for g in range(per)]
     scale = 1.0 / math.sqrt(rank)
     inverse = 1.0 / math.sqrt(dp * BLK)
@@ -77,6 +79,15 @@
     def when(condition, action):
         pl.when(condition)(action)
 
+    def send(make, u, *rest):
+        when(u >= RING, lambda: make(u - RING, *rest).wait_send())
+        make(u, *rest).start()
+
+    def send_piece(make, c, p):
+        back = RING // HALVES
+        when(c >= back, lambda: make(c - back, p).wait_send())
+        make(c, p).start()
+
     def to_dp(k):
         return {"dp": hops[k]}
 
@@ -93,7 +104,10 @@
     def w_copy(n):
         return pltpu.make_async_copy(w_hbm.at[:, tile_at(n)], w.at[:, tile_at(n)], w_sem.at[n])
 
-    tok_copy = pltpu.make_async_copy(tok_hbm, tok_in, in_sem.at[0])
+    lead = pl.ds(0, 2)
+    rest = pl.ds(2, CHUNKS - 2)
+    tok_lead = pltpu.make_async_copy(tok_hbm.at[:, lead], tok_in.at[:, lead], in_sem.at[0])
+    tok_rest = pltpu.make_async_copy(tok_hbm.at[:, rest], tok_in.at[:, rest], in_sem.at[4 + per])
     loads = [
         pltpu.make_async_copy(down_hbm, down, in_sem.at[1]),
         pltpu.make_async_copy(up_hbm, up, in_sem.at[2]),
@@ -113,7 +127,7 @@
         c = u // HALVES
         return copy(
             tok_in.at[:, c, :, lanes(h)], raw.at[c, :, :, lanes(h)],
-            s0_send.at[u], s0_recv.at[u], to_dp(0),
+            s0_send.at[u % RING], s0_recv.at[u % RING], to_dp(0),
         )
 
     def stage(k, u, h, owner):
@@ -121,19 +135,22 @@
         base = mirrored(owner, bits) // size * size
         rows = pl.ds(pl.multiple_of(base * ROWS, ROWS), size * ROWS)
         here = tok.at[u // HALVES, rows, lanes(h)]
-        return copy(here, here, st_send.at[k - 1, u], st_recv.at[k - 1, u], to_dp(k))
+        n = u % RING
+        return copy(here, here, st_send.at[k - 1, n], st_recv.at[k - 1, n], to_dp(k))
 
     def near_copy(c, p):
+        n = (c * HALVES + p) % RING
         start = (1 - core) * 2
         return copy(
             part.at[c, :, pl.ds(start, 2), :, span(p)], near.at[c, :, :, :, span(p)],
-            nr_send.at[c, p], nr_recv.at[c, p], near_id,
+            nr_send.at[n], nr_recv.at[n], near_id,
         )
 
     def far_copy(c, p):
+        n = (c * HALVES + p) % RING
         return copy(
             pair.at[c, :, :, span(p)], far.at[c, :, :, span(p)],
-            fr_send.at[c, p], fr_recv.at[c, p], far_id,
+            fr_send.at[n], fr_recv.at[n], far_id,
         )
 
     def home_copy(s):
@@ -192,6 +209,7 @@
         def _(n):
             body(tile_at(n))
 
+    tok_lead.start()
     barrier = pltpu.get_barrier_semaphore()
 
     def greet_dp(k):
@@ -204,7 +222,7 @@
     for k in range(1, tp):
         pl.semaphore_signal(barrier, inc=1, device_id={"tensor": (t + k) % tp}, device_id_type=MESH)
 
-    tok_copy.start()
+    tok_rest.start()
     for load in loads:
         load.start()
     for n in range(tiles):
@@ -213,10 +231,11 @@
         load.start()
 
     gm_acc[...] = jnp.zeros_like(gm_acc)
-    tok_copy.wait()
+    tok_lead.wait()
     pl.semaphore_wait(barrier, dp - 1 + tp - 1)
     for u in range(AHEAD):
         first(u, u % HALVES).start()
+    tok_rest.wait()
     for load in loads:
         load.wait()
 
@@ -298,7 +317,7 @@
             at = tile_at(n)
             prod = jnp.dot(tok[c], w[:, at], preferred_element_type=F32)
             part[c, :, :, :, at] = prod.astype(BF16).reshape(per, tp, ROWS, tile)
-        near_copy(c, p).start()
+        send_piece(near_copy, c, p)
 
     def combine(c, p):
         near_copy(c, p).wait_recv()
@@ -308,7 +327,7 @@
             pair[c, :, :, at] = (
                 part[c, :, other, :, at].astype(F32) + near[c, :, 1 - side, :, at].astype(F32)
             ).astype(BF16)
-        far_copy(c, p).start()
+        send_piece(far_copy, c, p)
 
     def epilogue(c, p):
         far_copy(c, p).wait_recv()
@@ -350,18 +369,17 @@
         norm_tile(n)
 
     later = max(0, tiles - EARLY)
-    norm_last = -(-later // 2)
-    grad_at = norm_last + 2
+    norm_last = max(1, later)
+    grad_at = norm_last + 8
     gap = max(1, (UNITS - grad_at) // (bits + 1))
-    ready = LAG * (bits - 1) + 1
-    steps = UNITS + ready + 1
-    steps = steps + steps % 2
-    gb_at = ready + 3
-
-    @pl.loop(0, steps // 2)
+    ready = LAG * (bits - 1) + HALVES - 1
+    steps = -(-(UNITS + ready + PAIR_LAG) // HALVES) * HALVES
+    gb_at = grad_at + 4
+
+    @pl.loop(0, steps // HALVES)
     def _(pass_):
-        for h in range(2):
-            u = pass_ * 2 + h
+        for h in range(HALVES):
+            u = pass_ * HALVES + h
 
             @pl.when(u < UNITS)
             def _():
@@ -372,30 +390,29 @@
                 pair_at = pl.ds(pl.multiple_of(mirrored(hops[0], bits) * ROWS, ROWS), ROWS)
                 tok[c, own_at, at] = jnp.where(own_live, tok_in[0, c, :, at], raw[c, 1, :, at])
                 tok[c, pair_at, at] = jnp.where(pair_live, raw[c, 0, :, at], tok_in[1, c, :, at])
-                stage(1, u, h, d).start()
-
-            when(u + AHEAD < UNITS, lambda: first(u + AHEAD, (h + AHEAD) % 2).start())
+                send(functools.partial(stage, 1), u, h, d)
+
+            when(u + AHEAD < UNITS, lambda: send(first, u + AHEAD, (h + AHEAD) % HALVES))
 
             for k in range(1, bits):
                 v = u - LAG * k
-                hv = (h - LAG * k) % 2
+                hv = (h - LAG * k) % HALVES
 
                 @pl.when((v >= 0) & (v < UNITS))
                 def _():
                     stage(k, v, hv, hops[k]).wait_recv()
                     if k < bits - 1:
-                        stage(k + 1, v, hv, d).start()
+                        send(functools.partial(stage, k + 1), v, hv, d)
 
             @pl.when((u >= 1) & (u <= norm_last))
             def _():
-                for e in range(2):
-                    n = EARLY + (u - 1) * 2 + e
-                    when(n < tiles, lambda: norm_tile(n))
-
-            when(u == 1, gather_down)
+                n = EARLY + u - 1
+                when(n < tiles, lambda: norm_tile(n))
+
+            when(u == 2, gather_down)
             when(u == norm_last, lambda: sq1.start())
 
-            @pl.when(u == norm_last + 1)
+            @pl.when(u == norm_last + 4)
             def _():
                 sq1.wait()
                 sq_near[...] = sq_near[...] + sq[...]
@@ -409,7 +426,7 @@
                 gradient()
                 rp_hops[0].start()
 
-            when(u == ready, take_down)
+            when(u == grad_at + 2, take_down)
 
             for k in range(bits):
                 @pl.when(u == grad_at + gap * (k + 1))
@@ -423,39 +440,43 @@
                         rgt[t] = merged.astype(BF16)
                         rg1.start()
 
-            @pl.when(u == grad_at + gap * bits + 1)
+            @pl.when(u == grad_at + gap * bits + 2)
             def _():
                 rg1.wait_send()
                 rg1_in.wait_recv()
                 rg2.start()
 
-            @pl.when(u == grad_at + gap * bits + 3)
+            @pl.when(u == grad_at + gap * bits + 6)
             def _():
                 rg2.wait_send()
                 rg2_in.wait_recv()
                 turn_rows()
 
             m = u - ready
-            hm = (h - ready) % 2
-            when((m >= 0) & (m < UNITS), lambda: multiply(m // 2, hm))
-            when((m >= 1) & (m <= UNITS), lambda: combine((m - 1) // 2, 1 - hm))
-            when((m >= 3) & (m <= UNITS), lambda: epilogue((m - 3) // 2, 1 - hm))
+            mq = m - PAIR_LAG
+            me = mq - END_LAG
+            at_m, at_q, at_e = (
+                (h - ready - lag) % HALVES for lag in (0, PAIR_LAG, PAIR_LAG + END_LAG)
+            )
+            when((m >= 0) & (m < UNITS), lambda: multiply(m // HALVES, at_m))
+            when((mq >= 0) & (mq < UNITS), lambda: combine(mq // HALVES, at_q))
+            when((me >= 0) & (me < UNITS - END_LAG), lambda: epilogue(me // HALVES, at_e))
 
             when(u == gb_at, gb_start)
 
-            @pl.when(u == gb_at + 2)
+            @pl.when(u == gb_at + 3)
             def _():
                 gb1.wait()
                 gb_sum[...] = (gb_part[core].astype(F32) + gb_near[...].astype(F32)).astype(BF16)
                 gb2.start()
 
-            @pl.when(u == gb_at + 6)
+            @pl.when(u == gb_at + 9)
             def _():
                 gb2.wait()
                 gb_all[core] = gb_sum[...].astype(F32) + gb_far[...].astype(F32)
                 gb3.start()
 
-            @pl.when(u == gb_at + 8)
+            @pl.when(u == gb_at + 12)
             def _():
                 gb3.wait_send()
                 gb3_in.wait_recv()
@@ -470,14 +491,14 @@
             rg_turned[...], tok[:, :, at].reshape(dp * BLK, wide), preferred_element_type=F32
         )
 
-    @pl.loop(0, CHUNKS)
+    @pl.loop(CHUNKS - RING // HALVES, CHUNKS)
     def _(c):
         for h in range(HALVES):
             u = c * HALVES + h
             first(u, h).wait_send()
             for k in range(1, bits):
                 stage(k, u, h, d).wait_send()
-        for p in range(2):
+        for p in range(HALVES):
             near_copy(c, p).wait_send()
 
     for s in range(2):
@@ -489,16 +510,16 @@
             def _(k):
                 spread(s, k).wait_send()
 
-    for q in range(UNITS - 2, UNITS):
-        epilogue(q // 2, q % 2)
+    for q in range(UNITS - END_LAG, UNITS):
+        epilogue(q // HALVES, q % HALVES)
 
     gm_in[t] = jnp.sum(gm_acc[...], axis=0, keepdims=True) / norm[...] * inverse
     for k in range(1, tp):
         gm_copy(k).start()
 
-    @pl.loop(0, CHUNKS)
+    @pl.loop(CHUNKS - RING // HALVES, CHUNKS)
     def _(c):
-        for p in range(2):
+        for p in range(HALVES):
             far_copy(c, p).wait_send()
 
     for k in range(1, tp):
@@ -583,12 +604,12 @@
             pltpu.VMEM((2, rank, BLK), BF16),
             pltpu.VMEM((2, tp, rank, BLK), BF16),
             pltpu.VMEM((2, dp, rank, BLK), BF16),
-            dma((4 + per,)),
+            dma((5 + per,)),
             dma((tiles,)),
-            dma((UNITS,)), dma((UNITS,)),
-            dma((bits - 1, UNITS)), dma((bits - 1, UNITS)),
-            dma((CHUNKS, 2)), dma((CHUNKS, 2)),
-            dma((CHUNKS, 2)), dma((CHUNKS, 2)),
+            dma((RING,)), dma((RING,)),
+            dma((bits - 1, RING)), dma((bits - 1, RING)),
+            dma((RING,)), dma((RING,)),
+            dma((RING,)), dma((RING,)),
             dma((bits + 7,)), dma((bits + 7,)),
             dma((2,)), dma((2, tp)),
             dma((dp,)), dma((2, dp)),

time: 85.6 us -> 79.9 us (0.933)
  Pallas kernels: 84.8 us -> 79.1 us
    pallas_call x1, Pallas kernels: 83.3 us -> 77.6 us  [body(): pl.pallas_call(functools.partial(kernel, cfg), out_shape=tuple((OUT(shape...]
where the time goes in v2:
time: 79.9 us; the launch traced here: 79.7 us
  Pallas kernels  79.1 us (99%)
    pallas_call x1, Pallas kernels, body(): pl.pallas_call(functools.partial(kernel, cfg), out_shape=tuple((OUT(shape...  77.6 us

profile of v2, /device:TPU:0, one launch (start us, length us, event | category | flops | bytes accessed | tf_op | source)
XLA Modules:
  0.0 79.7 jit_solution(14822449366131528250)
XLA Ops:
  0.6 77.6 %shard_map.102 = (bf16[2,128,3584]{2,1,0:T(8,128)(2,1)S(1)}, f32[32,2048]{1,0:T(8,128)S(1)}, f32[32,3584]{1,0:T(8,128)S(1)}, f32[3584]{0:T(1024)S(1)}) custom-call(bf16[2,8,16,2048]{3,2,1,0:T(8,128)(2,1)} %bitcast.5, s32[2,8]{1,0:T(2,128)} %bitcast.6, bf16[2048,3584]{1,0:T(8,128)(2,1)} %w_hbm.1, bf16[32,2048]{1,0:T(8,128)(2,1)} %down_hbm.1, ...), custom_call_target="tpu_custom_call" | custom-call | tf_op jit(solution)/shard_map/pallas_call | solution.py:566
  78.2 1.5 %shard_map.103 = (bf16[2,128,3584]{2,1,0:T(8,128)(2,1)}, f32[32,2048]{1,0:T(8,128)}, f32[32,3584]{1,0:T(8,128)}, f32[3584]{0:T(1024)}) custom-call(bf16[2,128,3584]{2,1,0:T(8,128)(2,1)S(1)} %get-tuple-element.12.out, f32[32,2048]{1,0:T(8,128)S(1)} %get-tuple-element.13.ga, f32[32,3584]{1,0:T(8,128)S(1)} %get-tuple-element.14.gb, f32[3584]{0:T(1024)S(1)} %get-tuple-element.15.gm), custom_call_target="tpu_custom_call" | custom-call | tf_op jit(solution)/shard_map/pallas_call | solution.py:631

commit v3 on v2

--- a/solution.py
+++ b/solution.py
@@ -18,7 +18,15 @@
 EARLY = 3
 PAIR_LAG = 1
 END_LAG = 4
-RING = HALVES * -(-(2 * max(AHEAD, LAG, PAIR_LAG, END_LAG) + 2) // HALVES)
+
+
+def ring(lag):
+    return HALVES * -(-(2 * lag + 2) // HALVES)
+
+
+RING = ring(max(AHEAD - 1, LAG))
+PAIR_RING = ring(PAIR_LAG)
+END_RING = ring(END_LAG)
 MESH = pl.DeviceIdType.MESH
 F32 = jnp.float32
 BF16 = jnp.bfloat16
@@ -83,8 +91,8 @@
         when(u >= RING, lambda: make(u - RING, *rest).wait_send())
         make(u, *rest).start()
 
-    def send_piece(make, c, p):
-        back = RING // HALVES
+    def send_piece(make, c, p, size):
+        back = size // HALVES
         when(c >= back, lambda: make(c - back, p).wait_send())
         make(c, p).start()
 
@@ -139,7 +147,7 @@
         return copy(here, here, st_send.at[k - 1, n], st_recv.at[k - 1, n], to_dp(k))
 
     def near_copy(c, p):
-        n = (c * HALVES + p) % RING
+        n = (c * HALVES + p) % PAIR_RING
         start = (1 - core) * 2
         return copy(
             part.at[c, :, pl.ds(start, 2), :, span(p)], near.at[c, :, :, :, span(p)],
@@ -147,7 +155,7 @@
         )
 
     def far_copy(c, p):
-        n = (c * HALVES + p) % RING
+        n = (c * HALVES + p) % END_RING
         return copy(
             pair.at[c, :, :, span(p)], far.at[c, :, :, span(p)],
             fr_send.at[n], fr_recv.at[n], far_id,
@@ -317,7 +325,7 @@
             at = tile_at(n)
             prod = jnp.dot(tok[c], w[:, at], preferred_element_type=F32)
             part[c, :, :, :, at] = prod.astype(BF16).reshape(per, tp, ROWS, tile)
-        send_piece(near_copy, c, p)
+        send_piece(near_copy, c, p, PAIR_RING)
 
     def combine(c, p):
         near_copy(c, p).wait_recv()
@@ -327,7 +335,7 @@
             pair[c, :, :, at] = (
                 part[c, :, other, :, at].astype(F32) + near[c, :, 1 - side, :, at].astype(F32)
             ).astype(BF16)
-        send_piece(far_copy, c, p)
+        send_piece(far_copy, c, p, END_RING)
 
     def epilogue(c, p):
         far_copy(c, p).wait_recv()
@@ -498,6 +506,9 @@
             first(u, h).wait_send()
             for k in range(1, bits):
                 stage(k, u, h, d).wait_send()
+
+    @pl.loop(CHUNKS - PAIR_RING // HALVES, CHUNKS)
+    def _(c):
         for p in range(HALVES):
             near_copy(c, p).wait_send()
 
@@ -517,7 +528,7 @@
     for k in range(1, tp):
         gm_copy(k).start()
 
-    @pl.loop(CHUNKS - RING // HALVES, CHUNKS)
+    @pl.loop(CHUNKS - END_RING // HALVES, CHUNKS)
     def _(c):
         for p in range(HALVES):
             far_copy(c, p).wait_send()
@@ -608,8 +619,8 @@
             dma((tiles,)),
             dma((RING,)), dma((RING,)),
             dma((bits - 1, RING)), dma((bits - 1, RING)),
-            dma((RING,)), dma((RING,)),
-            dma((RING,)), dma((RING,)),
+            dma((PAIR_RING,)), dma((PAIR_RING,)),
+            dma((END_RING,)), dma((END_RING,)),
             dma((bits + 7,)), dma((bits + 7,)),
             dma((2,)), dma((2, tp)),
             dma((dp,)), dma((2, dp)),

time: 79.9 us -> 79.6 us (level)
  no operation moved by 1% of the time
where the time goes in v3:
time: 79.6 us; the launch traced here: 79.4 us
  Pallas kernels  78.8 us (99%)
    pallas_call x1, Pallas kernels, body(): pl.pallas_call(functools.partial(kernel, cfg), out_shape=tuple((OUT(shape...  77.2 us

profile of v3, /device:TPU:0, one launch (start us, length us, event | category | flops | bytes accessed | tf_op | source)
XLA Modules:
  0.0 79.4 jit_solution(6547273590674386374)
XLA Ops:
  0.6 77.2 %shard_map.102 = (bf16[2,128,3584]{2,1,0:T(8,128)(2,1)S(1)}, f32[32,2048]{1,0:T(8,128)S(1)}, f32[32,3584]{1,0:T(8,128)S(1)}, f32[3584]{0:T(1024)S(1)}) custom-call(bf16[2,8,16,2048]{3,2,1,0:T(8,128)(2,1)} %bitcast.5, s32[2,8]{1,0:T(2,128)} %bitcast.6, bf16[2048,3584]{1,0:T(8,128)(2,1)} %w_hbm.1, bf16[32,2048]{1,0:T(8,128)(2,1)} %down_hbm.1, ...), custom_call_target="tpu_custom_call" | custom-call | tf_op jit(solution)/shard_map/pallas_call | solution.py:577
  77.9 1.5 %shard_map.103 = (bf16[2,128,3584]{2,1,0:T(8,128)(2,1)}, f32[32,2048]{1,0:T(8,128)}, f32[32,3584]{1,0:T(8,128)}, f32[3584]{0:T(1024)}) custom-call(bf16[2,128,3584]{2,1,0:T(8,128)(2,1)S(1)} %get-tuple-element.12.out, f32[32,2048]{1,0:T(8,128)S(1)} %get-tuple-element.13.ga, f32[32,3584]{1,0:T(8,128)S(1)} %get-tuple-element.14.gb, f32[3584]{0:T(1024)S(1)} %get-tuple-element.15.gm), custom_call_target="tpu_custom_call" | custom-call | tf_op jit(solution)/shard_map/pallas_call | solution.py:642
